TPU v7x, 256 devices: a whole 4x4x8 slice. The times are simulated.
256 devices in a mesh: tp: 8 (over z_lo, x), dp: 8 (over y, core), rep: 4 (over z_hi).
Axes of the slice: x: 4, y: 4, z: 8 (z_hi: 4, z_lo: 2; z = z_hi * 2 + z_lo), core: 2. Of those that a mesh axis runs over, the one named last changes fastest.
Arguments:
- prompts: bfloat16 [24576, 8192], P(('dp', 'rep'), 'tp'), may hold values from -6 to 6
- frozen_projection_weight: bfloat16 [2, 8192, 2048], P(None, ('dp', 'rep'), 'tp'), may hold values from -5 to 5
- lowrank_down_factor: bfloat16 [2, 8192, 64], P(None, ('dp', 'rep')), may hold values from -0.119628906 to 0.119628906
- lowrank_up_factor: bfloat16 [2, 64, 2048], P(None, None, 'tp'), may hold values from -0.59765625 to 0.59765625
- magnitude: float32 [2, 2048], P(None, 'tp'), may hold values from 0.5 to 2
Outputs:
- key_values: bfloat16 [2, 24576, 2048], P(None, ('dp', 'rep'), 'tp')
All inputs are finite; a program needn't handle non-finite values.
Results may differ from a plain program's by a relative error of at most 0.0049.
Values may be sent and summed in bfloat16 or wider, within the bound.
No kernel may reach another device: no remote copies, remote signals or barrier semaphores. Data moves between devices by JAX's collectives and lax.ppermute only.
A program may use at most 64 MiB of HBM per device.

v0:
```python
import functools
import jax
import jax.numpy as jnp
from jax import lax
from jax.sharding import Mesh
from jax.sharding import PartitionSpec as P

DP_REP = ("dp_0", "dp_1", "rep")
epsilon = 1e-06


def one_axis_at_a_time(array, axes):
    return functools.reduce(lax.psum, axes, array)


def combine_weight_rows(weight_rows, down_rows, up_matrix):
    return weight_rows.astype(jnp.float32) + jnp.dot(
        down_rows, up_matrix, preferred_element_type=jnp.float32
    )


def prefilled_shard_values(
    frozen_projection_weight, lowrank_down_factor, lowrank_up_factor, magnitude, current_layer_index
):
    combined_weight = combine_weight_rows(
        frozen_projection_weight[current_layer_index],
        lowrank_down_factor[current_layer_index],
        lowrank_up_factor[current_layer_index],
    )
    squares = one_axis_at_a_time(jnp.sum(combined_weight * combined_weight, axis=0), DP_REP)
    factor = magnitude[current_layer_index] / jnp.sqrt(squares + epsilon)
    return (combined_weight * factor).astype(jnp.bfloat16)


def local(prompts, frozen_projection_weight, lowrank_down_factor, lowrank_up_factor, magnitude):
    layer_total = frozen_projection_weight.shape[0]
    features = lax.all_gather(prompts, "tp", axis=1, tiled=True)
    outputs = []
    for current_layer_index in range(layer_total):
        prefilled_key_values = prefilled_shard_values(
            frozen_projection_weight,
            lowrank_down_factor,
            lowrank_up_factor,
            magnitude,
            current_layer_index,
        )
        result = jnp.dot(
            features,
            lax.all_gather(prefilled_key_values, DP_REP, axis=0, tiled=True),
            preferred_element_type=jnp.float32,
        )
        outputs.append(result.astype(jnp.bfloat16))
    return jnp.stack(outputs)


def solution(mesh):
    split = Mesh(
        mesh.devices.reshape(mesh.shape["tp"], 4, 2, mesh.shape["rep"]),
        ("tp", "dp_0", "dp_1", "rep"),
    )
    in_specs = (
        P(DP_REP, "tp"),
        P(None, DP_REP, "tp"),
        P(None, DP_REP, None),
        P(None, None, "tp"),
        P(None, "tp"),
    )
    out_specs = P(None, DP_REP, "tp")
    return jax.shard_map(local, mesh=split, in_specs=in_specs, out_specs=out_specs, check_vma=False)
```

profile of v0, /device:TPU:1, one launch (start us, length us, event | category | flops | bytes accessed | tf_op | source)
XLA Modules:
  0.0 308.4 jit_solution(7998691284493703192)
XLA Ops:
  6.5 0.0 all-gather.4.cloned.1.call-start
  6.5 1.2 multiply_reduce_fusion
  7.7 1.2 multiply_reduce_fusion.1
  8.9 0.8 fusion.10
  9.7 9.5 %all-reduce.1 = (f32[256]{0:T(256)S(1)}, f32[256]{0:T(256)S(1)}) all-reduce(f32[256]{0:T(256)S(1)} %get-tuple-element.13, f32[256]{0:T(256)S(1)} %get-tuple-element.15), channel_id=1, replica_groups=mesh['tp'=8,'dp_0'=4,'dp_1'=2,'rep'=4] {'dp_0'}, use_global_device_ids=true, to_apply=%region_5.0 | all-reduce | flops 512 | bytes 4096 | tf_op jit(solution)/shard_map/psum | solution.py:13
  19.2 4.8 %all-reduce.2 = (f32[256]{0:T(256)S(1)}, f32[256]{0:T(256)S(1)}) all-reduce(f32[256]{0:T(256)S(1)} %get-tuple-element.7, f32[256]{0:T(256)S(1)} %get-tuple-element.8), channel_id=1, replica_groups=mesh['tp'=8,'dp_0'=4,'dp_1'=2,'rep'=4] {'dp_1'}, use_global_device_ids=true, to_apply=%region_6.0 | all-reduce | flops 512 | bytes 4096 | tf_op jit(solution)/shard_map/psum | solution.py:13
  24.0 12.9 %all-reduce = (f32[256]{0:T(256)S(1)}, f32[256]{0:T(256)S(1)}) all-reduce(f32[256]{0:T(256)S(1)} %get-tuple-element.9, f32[256]{0:T(256)S(1)} %get-tuple-element.10), channel_id=1, replica_groups=mesh['tp'=8,'dp_0'=4,'dp_1'=2,'rep'=4] {'rep'}, use_global_device_ids=true, to_apply=%region_7.0 | all-reduce | flops 512 | bytes 4096 | tf_op jit(solution)/shard_map/psum | solution.py:13
  36.9 0.7 multiply_convert_fusion.1
  37.6 0.0 all-gather.4.cloned.1.call-update
  37.6 0.0 all-gather.6.cloned.1.call-start
  37.6 0.7 all-gather.6.cloned.1.call-update
  38.3 0.0 all-gather.8.cloned.1.call-start
  38.4 0.7 multiply_convert_fusion
  39.1 0.0 all-gather.8.cloned.1.call-update
  39.1 56.9 %all-gather.4.cloned.1.call-done = bf16[8192,256]{1,0:T(8,128)(2,1)} async-done(((bf16[256,256]{1,0:T(8,128)(2,1)}), bf16[8192,256]{1,0:T(8,128)(2,1)}) %all-gather.4.cloned.1.call-update) | async-done | bytes 4194320 | tf_op jit(solution)/shard_map/all_gather | solution.py:49
  96.0 133.1 %all-gather.6.cloned.1.call-done = bf16[768,8192]{1,0:T(8,128)(2,1)} async-done(((bf16[768,1024]{1,0:T(8,128)(2,1)}), bf16[768,8192]{1,0:T(8,128)(2,1)}) %all-gather.6.cloned.1.call-update) | async-done | bytes 12582928 | tf_op jit(solution)/shard_map/all_gather | solution.py:37
  229.1 9.3 %fusion = bf16[1,768,256]{1,2,0:T(8,128)(2,1)S(1)} fusion(bf16[8192,256]{1,0:T(8,128)(2,1)} %all-gather.4.cloned.1.call-done, bf16[768,8192]{1,0:T(8,128)(2,1)} %all-gather.6.cloned.1.call-done), kind=kOutput, calls=%fused_computation.2 | convolution fusion | flops 3221422080 | bytes 17170432 | tf_op jit(solution)/shard_map/dot_general | solution.py:47
  238.4 52.9 %all-gather.8.cloned.1.call-done = bf16[8192,256]{1,0:T(8,128)(2,1)} async-done(((bf16[256,256]{1,0:T(8,128)(2,1)}), bf16[8192,256]{1,0:T(8,128)(2,1)}) %all-gather.8.cloned.1.call-update) | async-done | bytes 4194320 | tf_op jit(solution)/shard_map/all_gather | solution.py:49
  291.3 9.3 %fusion.1 = bf16[1,768,256]{1,2,0:T(8,128)(2,1)S(1)} fusion(bf16[8192,256]{1,0:T(8,128)(2,1)} %all-gather.8.cloned.1.call-done, bf16[768,8192]{1,0:T(8,128)(2,1)} %all-gather.6.cloned.1.call-done), kind=kOutput, calls=%fused_computation.3 | convolution fusion | flops 3221422080 | bytes 17170432 | tf_op jit(solution)/shard_map/dot_general | solution.py:47
  300.7 0.1 pad_maximum_fusion
  300.8 1.2 copy.6
  (2 shorter events, 0.0 us)
Async XLA Ops:
  6.5 89.5 %all-gather.4.cloned.1.call-start = ((), (), s32[]{:S(2)}) async-start(), calls=%async_computation | async-start | bytes 4325376 | tf_op jit(solution)/shard_map/all_gather | solution.py:49
  37.6 191.5 %all-gather.6.cloned.1.call-start = ((), (), s32[]{:S(2)}) async-start(), calls=%async_computation.1 | async-start | bytes 14155776 | tf_op jit(solution)/shard_map/all_gather | solution.py:37
  38.3 253.0 %all-gather.8.cloned.1.call-start = ((), (), s32[]{:S(2)}) async-start(), calls=%async_computation.2 | async-start | bytes 4325376 | tf_op jit(solution)/shard_map/all_gather | solution.py:49
Sparse Core Ops, SparseCore 0:
  37.7 58.2 all-gather.3
  97.8 131.2 all-gather.5
  231.6 59.6 all-gather.7
where the time goes:
time: 309 us; the launch traced here: 308 us
  waiting for transfers between devices  244 us (79%)
  blocking collectives  27.2 us (9%)
  matrix products  21 us (7%)
  between operations  13.1 us (4%)
    all_gather x1, waiting for transfers between devices, local(): features = lax.all_gather(prompts, 'tp', axis=1, tiled=True)  133 us
    all_gather x2, waiting for transfers between devices, local(): lax.all_gather(prefilled_key_values, DP_REP, axis=0, tiled=True)  110 us
    psum x3, blocking collectives, one_axis_at_a_time(): return functools.reduce(lax.psum, axes, array)  27.2 us
    dot_general x2, matrix products, local(): jnp.dot(features, lax.all_gather(prefilled_key_values, DP_REP, axis=0, ti...  18.6 us
  transfers between devices with their start and end apart: 3, of which 3 were waited for; matrix products, arithmetic and copies ran while one was open for 3% of the time, Pallas kernels for 0%

commit v1 on v0

--- a/solution.py
+++ b/solution.py
@@ -4,9 +4,17 @@
 from jax import lax
 from jax.sharding import Mesh
 from jax.sharding import PartitionSpec as P
+from jax.lax import all_to_all, psum
 
 DP_REP = ("dp_0", "dp_1", "rep")
 epsilon = 1e-06
+
+
+def derive_the_scenes(v0, comm_axis):
+    odd = jnp.stack([v0 for _ in range(psum(1, comm_axis))])
+    outcome_arr = all_to_all(odd, comm_axis, 0, 0)
+    r2 = jnp.concatenate(outcome_arr, axis=0)
+    return r2
 
 
 def one_axis_at_a_time(array, axes):
@@ -46,7 +54,7 @@
         )
         result = jnp.dot(
             features,
-            lax.all_gather(prefilled_key_values, DP_REP, axis=0, tiled=True),
+            derive_the_scenes(prefilled_key_values, DP_REP),
             preferred_element_type=jnp.float32,
         )
         outputs.append(result.astype(jnp.bfloat16))

time: 309 us -> 346 us (1.12)
  waiting for transfers between devices: 244 us -> 263 us
  starting transfers between devices: 0.08 us -> 12.3 us
  local copies, waits for them, and re-layouts: 1.92 us -> 6.79 us
    all_to_all x0 -> x2, waiting for transfers between devices: none -> 146 us  [derive_the_scenes(): outcome_arr = all_to_all(odd, comm_axis, 0, 0)]
    all_gather x2 -> x0, waiting for transfers between devices: 110 us -> none  [local(): lax.all_gather(prefilled_key_values, DP_REP, axis=0, tiled=True)]
    all_gather x1, waiting for transfers between devices: 133 us -> 117 us  [local(): features = lax.all_gather(prompts, 'tp', axis=1, tiled=True)]
    all_to_all x0 -> x2, starting transfers between devices: none -> 12.3 us  [derive_the_scenes(): outcome_arr = all_to_all(odd, comm_axis, 0, 0)]
    another operation x0 -> x2, local copies, waits for them, and re-layouts: none -> 4.87 us  [derive_the_scenes(): odd = jnp.stack([v0 for _ in range(psum(1, comm_axis))])]
  transfers between devices with their start and end apart: 3 -> 3, of which waited for: 3 -> 3; matrix products, arithmetic and copies ran while one was open for 3% -> 5% of each run, Pallas kernels for 0% -> 0%
where the time goes in v1:
time: 346 us; the launch traced here: 345 us
  waiting for transfers between devices  263 us (76%)
  blocking collectives  28.2 us (8%)
  matrix products  21 us (6%)
  between operations  13.5 us (4%)
  starting transfers between devices  12.3 us (4%)
  local copies, waits for them, and re-layouts  6.79 us (2%)
    all_to_all x2, waiting for transfers between devices, derive_the_scenes(): outcome_arr = all_to_all(odd, comm_axis, 0, 0)  146 us
    all_gather x1, waiting for transfers between devices, local(): features = lax.all_gather(prompts, 'tp', axis=1, tiled=True)  117 us
    psum x3, blocking collectives, one_axis_at_a_time(): return functools.reduce(lax.psum, axes, array)  28.2 us
    dot_general x2, matrix products, local(): jnp.dot(features, derive_the_scenes(prefilled_key_values, DP_REP), prefer...  18.6 us
    all_to_all x2, starting transfers between devices, derive_the_scenes(): outcome_arr = all_to_all(odd, comm_axis, 0, 0)  12.3 us
  transfers between devices with their start and end apart: 3, of which 3 were waited for; matrix products, arithmetic and copies ran while one was open for 5% of the time, Pallas kernels for 0%

profile of v1, /device:TPU:1, one launch (start us, length us, event | category | flops | bytes accessed | tf_op | source)
XLA Modules:
  0.0 345.3 jit_solution(5600731911941736502)
XLA Ops:
  6.5 0.0 all-gather.2.cloned.1.call-start
  6.5 0.7 all-gather.2.cloned.1.call-update
  7.3 1.2 multiply_reduce_fusion
  8.4 1.2 multiply_reduce_fusion.1
  9.6 9.5 %all-reduce.1 = (f32[256]{0:T(256)S(1)}, f32[256]{0:T(256)S(1)}) all-reduce(f32[256]{0:T(256)S(1)} %get-tuple-element.13, f32[256]{0:T(256)S(1)} %get-tuple-element.15), channel_id=1, replica_groups=mesh['tp'=8,'dp_0'=4,'dp_1'=2,'rep'=4] {'dp_0'}, use_global_device_ids=true, to_apply=%region_5.0 | all-reduce | flops 512 | bytes 4096 | tf_op jit(solution)/shard_map/psum | solution.py:21
  19.2 4.8 %all-reduce.2 = (f32[256]{0:T(256)S(1)}, f32[256]{0:T(256)S(1)}) all-reduce(f32[256]{0:T(256)S(1)} %get-tuple-element.7, f32[256]{0:T(256)S(1)} %get-tuple-element.8), channel_id=1, replica_groups=mesh['tp'=8,'dp_0'=4,'dp_1'=2,'rep'=4] {'dp_1'}, use_global_device_ids=true, to_apply=%region_6.0 | all-reduce | flops 512 | bytes 4096 | tf_op jit(solution)/shard_map/psum | solution.py:21
  24.0 13.9 %all-reduce = (f32[256]{0:T(256)S(1)}, f32[256]{0:T(256)S(1)}) all-reduce(f32[256]{0:T(256)S(1)} %get-tuple-element.9, f32[256]{0:T(256)S(1)} %get-tuple-element.10), channel_id=1, replica_groups=mesh['tp'=8,'dp_0'=4,'dp_1'=2,'rep'=4] {'rep'}, use_global_device_ids=true, to_apply=%region_7.0 | all-reduce | flops 512 | bytes 4096 | tf_op jit(solution)/shard_map/psum | solution.py:21
  37.9 0.8 fusion.10
  38.7 2.4 stack.12
  41.1 6.1 %all-to-all-start.1 = ((bf16[32,256,256]{2,1,0:T(8,128)(2,1)}), bf16[32,256,256]{2,1,0:T(8,128)(2,1)}, u32[]{:S(2)}, u32[]{:S(2)}) async-start(bf16[32,256,256]{2,1,0:T(8,128)(2,1)} %stack.12), calls=%async_computation.1 | async-start | bytes 8388608 | tf_op jit(solution)/shard_map/all_to_all | solution.py:15
  47.3 140.6 %all-to-all-done.1 = bf16[32,256,256]{2,1,0:T(8,128)(2,1)} async-done(((bf16[32,256,256]{2,1,0:T(8,128)(2,1)}), bf16[32,256,256]{2,1,0:T(8,128)(2,1)}, u32[]{:S(2)}, u32[]{:S(2)}) %all-to-all-start.1) | async-done | bytes 4194336 | tf_op jit(solution)/shard_map/all_to_all | solution.py:15
  187.9 2.4 stack.10
  190.3 6.2 %all-to-all-start = ((bf16[32,256,256]{2,1,0:T(8,128)(2,1)}), bf16[32,256,256]{2,1,0:T(8,128)(2,1)}, u32[]{:S(2)}, u32[]{:S(2)}) async-start(bf16[32,256,256]{2,1,0:T(8,128)(2,1)} %stack.10), calls=%async_computation | async-start | bytes 8388608 | tf_op jit(solution)/shard_map/all_to_all | solution.py:15
  196.5 117.0 %all-gather.2.cloned.1.call-done = bf16[768,8192]{1,0:T(8,128)(2,1)} async-done(((bf16[768,1024]{1,0:T(8,128)(2,1)}), bf16[768,8192]{1,0:T(8,128)(2,1)}) %all-gather.2.cloned.1.call-update) | async-done | bytes 12582928 | tf_op jit(solution)/shard_map/all_gather | solution.py:45
  313.5 9.3 %fusion.1 = bf16[1,768,256]{1,2,0:T(8,128)(2,1)S(1)} fusion(bf16[8192,256]{1,0:T(8,128)(2,1)} %bitcast.11, bf16[768,8192]{1,0:T(8,128)(2,1)} %all-gather.2.cloned.1.call-done), kind=kOutput, calls=%fused_computation.3 | convolution fusion | flops 3221422080 | bytes 17170432 | tf_op jit(solution)/shard_map/dot_general | solution.py:55
  322.9 5.0 %all-to-all-done = bf16[32,256,256]{2,1,0:T(8,128)(2,1)} async-done(((bf16[32,256,256]{2,1,0:T(8,128)(2,1)}), bf16[32,256,256]{2,1,0:T(8,128)(2,1)}, u32[]{:S(2)}, u32[]{:S(2)}) %all-to-all-start) | async-done | bytes 4194336 | tf_op jit(solution)/shard_map/all_to_all | solution.py:15
  327.8 9.3 %fusion = bf16[1,768,256]{1,2,0:T(8,128)(2,1)S(1)} fusion(bf16[8192,256]{1,0:T(8,128)(2,1)} %bitcast.4, bf16[768,8192]{1,0:T(8,128)(2,1)} %all-gather.2.cloned.1.call-done), kind=kOutput, calls=%fused_computation.2 | convolution fusion | flops 3221422080 | bytes 17170432 | tf_op jit(solution)/shard_map/dot_general | solution.py:55
  337.2 0.1 pad_maximum_fusion
  337.3 1.2 copy.6
  (3 shorter events, 0.1 us)
Async XLA Ops:
  6.5 307.0 %all-gather.2.cloned.1.call-start = ((), (), s32[]{:S(2)}) async-start(), calls=%async_computation.2 | async-start | bytes 14155776 | tf_op jit(solution)/shard_map/all_gather | solution.py:45
  41.1 146.8 %all-to-all-start.1 = ((bf16[32,256,256]{2,1,0:T(8,128)(2,1)}), bf16[32,256,256]{2,1,0:T(8,128)(2,1)}, u32[]{:S(2)}, u32[]{:S(2)}) async-start(bf16[32,256,256]{2,1,0:T(8,128)(2,1)} %stack.12), calls=%async_computation.1 | async-start | bytes 8388608 | tf_op jit(solution)/shard_map/all_to_all | solution.py:15
  190.3 137.5 %all-to-all-start = ((bf16[32,256,256]{2,1,0:T(8,128)(2,1)}), bf16[32,256,256]{2,1,0:T(8,128)(2,1)}, u32[]{:S(2)}, u32[]{:S(2)}) async-start(bf16[32,256,256]{2,1,0:T(8,128)(2,1)} %stack.10), calls=%async_computation | async-start | bytes 8388608 | tf_op jit(solution)/shard_map/all_to_all | solution.py:15
Sparse Core Ops, SparseCore 0:
  9.1 304.3 all-gather.1
